TPU v7x, 16 devices: a whole 2x2x2 slice. The times are simulated.
16 devices in a mesh: ep: 16 (over z, y, x, core).
Axes of the slice: x: 2, y: 2, z: 2, core: 2. Of those that a mesh axis runs over, the one named last changes fastest.
Arguments:
- hidden: bfloat16 [32768, 1280], P('ep')
- grad_out: bfloat16 [32768, 1280], P('ep')
- routes: int32 [32768, 6], P('ep')
- w_router: bfloat16 [1280, 64], replicated
- w_one: bfloat16 [64, 1280, 896], P('ep')
- w_three: bfloat16 [64, 1280, 896], P('ep')
- w_two: bfloat16 [64, 896, 1280], P('ep')
- shared_one: bfloat16 [1280, 1792], replicated
- shared_three: bfloat16 [1280, 1792], replicated
- shared_two: bfloat16 [1792, 1280], replicated
Outputs:
- output 1: bfloat16 [32768, 1280], P('ep')
- output 2: bfloat16 [32768, 1280], P('ep')
- output 3: float32 [1280, 64], replicated
- output 4: bfloat16 [64, 1280, 896], P('ep')
- output 5: bfloat16 [64, 1280, 896], P('ep')
- output 6: bfloat16 [64, 896, 1280], P('ep')
- output 7: float32 [1280, 1792], replicated
- output 8: float32 [1280, 1792], replicated
- output 9: float32 [1792, 1280], replicated
All inputs are finite; a program needn't handle non-finite values.
Results may differ from a plain program's by a relative error of at most 0.00199.
Values are sent between devices in bfloat16 or wider.
A program may use at most 1 GiB of HBM per device.

v0:
```python
import jax
import jax.numpy as jnp
from jax import lax
from jax.sharding import PartitionSpec as P

ROUTE_SCALE = 2.5


def silu_parts(pre_act):
    sig_val = jax.nn.sigmoid(pre_act)
    return pre_act * sig_val, sig_val * (1.0 + pre_act * (1.0 - sig_val))


def router_weights(hidden, routes, w_router):
    logits = jnp.dot(hidden, w_router, preferred_element_type=jnp.float32)
    picked = jnp.take_along_axis(jax.nn.sigmoid(logits), routes, axis=1)
    pick_sum = jnp.sum(picked, axis=1, keepdims=True)
    return picked, pick_sum, ROUTE_SCALE * picked / pick_sum


def slot_tables(routes, weights, num_experts, capacity):
    tok_count = routes.shape[0]
    expert_ids = jnp.arange(num_experts, dtype=jnp.int32)
    hit_count = jnp.sum((routes[:, :, None] == expert_ids).astype(jnp.int32), axis=1)
    before = jnp.cumsum(hit_count, axis=0) - hit_count
    position = jnp.take_along_axis(before, routes, axis=1)
    slot_ids = jnp.where(position < capacity, routes * capacity + position, num_experts * capacity)
    token_ids = jnp.broadcast_to(jnp.arange(tok_count, dtype=jnp.int32)[:, None], routes.shape)
    flat_slots = slot_ids.reshape(-1)
    slot_token = jnp.full((num_experts * capacity,), tok_count, jnp.int32).at[flat_slots].set(token_ids.reshape(-1), mode='drop')
    slot_weight = jnp.zeros((num_experts * capacity,), jnp.float32).at[flat_slots].set(weights.reshape(-1), mode='drop')
    return slot_ids, slot_token, slot_weight


def router_grad_logits(route_dot, picked, pick_sum, weights, routes, num_experts):
    mean_term = jnp.sum(route_dot * weights, axis=1, keepdims=True) / ROUTE_SCALE
    grad_pick = ROUTE_SCALE / pick_sum * (route_dot - mean_term) * picked * (1.0 - picked)
    is_choice = routes[:, :, None] == jnp.arange(num_experts, dtype=jnp.int32)
    return jnp.sum(jnp.where(is_choice, grad_pick[:, :, None], 0.0), axis=1).astype(jnp.bfloat16)


def shared_forward(hidden, shared_one, shared_three, shared_two):
    pre_one = jnp.dot(hidden, shared_one, preferred_element_type=jnp.float32)
    pre_three = jnp.dot(hidden, shared_three, preferred_element_type=jnp.float32)
    act_one, dact_one = silu_parts(pre_one)
    mid_act = (act_one * pre_three).astype(jnp.bfloat16)
    return jnp.dot(mid_act, shared_two, preferred_element_type=jnp.float32), (pre_three, act_one, dact_one, mid_act)


def shared_backward(hidden, grad_out, saved_acts, shared_one, shared_three, shared_two):
    pre_three, act_one, dact_one, mid_act = saved_acts
    grad_mid = jnp.einsum('td,fd->tf', grad_out, shared_two, preferred_element_type=jnp.float32)
    grad_one = (grad_mid * pre_three * dact_one).astype(jnp.bfloat16)
    grad_three = (grad_mid * act_one).astype(jnp.bfloat16)
    wgrad_one = jnp.einsum('td,tf->df', hidden, grad_one, preferred_element_type=jnp.float32)
    wgrad_three = jnp.einsum('td,tf->df', hidden, grad_three, preferred_element_type=jnp.float32)
    wgrad_two = jnp.einsum('tf,td->fd', mid_act, grad_out, preferred_element_type=jnp.float32)
    dx_part = jnp.einsum('tf,df->td', grad_one, shared_one, preferred_element_type=jnp.float32) + jnp.einsum('tf,df->td', grad_three, shared_three, preferred_element_type=jnp.float32)
    return dx_part, wgrad_one, wgrad_three, wgrad_two


def expert_forward(in_rows, w_one, w_three, w_two):
    pre_one = jnp.einsum('secd,edf->secf', in_rows, w_one, preferred_element_type=jnp.float32)
    pre_three = jnp.einsum('secd,edf->secf', in_rows, w_three, preferred_element_type=jnp.float32)
    act_one, dact_one = silu_parts(pre_one)
    mid_act = (act_one * pre_three).astype(jnp.bfloat16)
    expert_out = jnp.einsum('secf,efd->secd', mid_act, w_two, preferred_element_type=jnp.float32).astype(jnp.bfloat16)
    return expert_out, (pre_three, act_one, dact_one, mid_act)


def expert_backward(in_rows, grad_rows, saved_acts, w_one, w_three, w_two):
    pre_three, act_one, dact_one, mid_act = saved_acts
    grad_mid = jnp.einsum('secd,efd->secf', grad_rows, w_two, preferred_element_type=jnp.float32)
    grad_one = (grad_mid * pre_three * dact_one).astype(jnp.bfloat16)
    grad_three = (grad_mid * act_one).astype(jnp.bfloat16)
    wgrad_two = jnp.einsum('secf,secd->efd', mid_act, grad_rows, preferred_element_type=jnp.float32)
    wgrad_one = jnp.einsum('secd,secf->edf', in_rows, grad_one, preferred_element_type=jnp.float32)
    wgrad_three = jnp.einsum('secd,secf->edf', in_rows, grad_three, preferred_element_type=jnp.float32)
    dx_rows = (jnp.einsum('secf,edf->secd', grad_one, w_one, preferred_element_type=jnp.float32) + jnp.einsum('secf,edf->secd', grad_three, w_three, preferred_element_type=jnp.float32)).astype(jnp.bfloat16)
    return dx_rows, wgrad_one, wgrad_three, wgrad_two


def solution(mesh):
    group_size = mesh.shape['ep']
    row_spec = P('ep', None)
    expert_spec = P('ep', None, None)
    copy_spec = P()

    def local_step(hidden, grad_out, routes, w_router, w_one, w_three, w_two, shared_one, shared_three, shared_two):
        tok_count, d_model = hidden.shape
        top_k = routes.shape[1]
        num_experts = w_router.shape[1]
        local_experts = w_one.shape[0]
        capacity = (5 * tok_count * top_k + 4 * num_experts - 1) // (4 * num_experts)
        buffer_shape = (group_size, local_experts, capacity, d_model)
        flat_shape = (num_experts * capacity, d_model)
        picked, pick_sum, weights = router_weights(hidden, routes, w_router)
        slot_ids, slot_token, slot_weight = slot_tables(routes, weights, num_experts, capacity)
        send_rows = jnp.take(hidden, slot_token, axis=0, mode='fill', fill_value=0).reshape(buffer_shape)
        recv_rows = lax.all_to_all(send_rows, 'ep', 0, 0)
        expert_out, expert_saved = expert_forward(recv_rows, w_one, w_three, w_two)
        back_rows = lax.all_to_all(expert_out, 'ep', 0, 0).reshape(flat_shape)
        gathered = jnp.take(back_rows, slot_ids, axis=0, mode='fill', fill_value=0)
        routed = jnp.sum(weights[:, :, None] * gathered, axis=1)
        shared_out, shared_saved = shared_forward(hidden, shared_one, shared_three, shared_two)
        hidden_out = (hidden.astype(jnp.float32) + shared_out + routed).astype(jnp.bfloat16)
        grad_rows = jnp.take(grad_out, slot_token, axis=0, mode='fill', fill_value=0)
        grad_send = (slot_weight[:, None] * grad_rows).astype(jnp.bfloat16).reshape(buffer_shape)
        grad_recv = lax.all_to_all(grad_send, 'ep', 0, 0)
        dx_rows, wgrad_one, wgrad_three, wgrad_two = expert_backward(recv_rows, grad_recv, expert_saved, w_one, w_three, w_two)
        dx_back = lax.all_to_all(dx_rows, 'ep', 0, 0).reshape(flat_shape)
        dx_routed = jnp.sum(jnp.take(dx_back, slot_ids, axis=0, mode='fill', fill_value=0), axis=1, dtype=jnp.float32)
        shared_dx, sgrad_one, sgrad_three, sgrad_two = shared_backward(hidden, grad_out, shared_saved, shared_one, shared_three, shared_two)
        route_dot = jnp.einsum('td,tkd->tk', grad_out, gathered, preferred_element_type=jnp.float32)
        grad_logits = router_grad_logits(route_dot, picked, pick_sum, weights, routes, num_experts)
        router_part = jnp.einsum('td,te->de', hidden, grad_logits, preferred_element_type=jnp.float32)
        gate_dx = jnp.einsum('te,de->td', grad_logits, w_router, preferred_element_type=jnp.float32)
        grad_hidden = (grad_out.astype(jnp.float32) + shared_dx + gate_dx + dx_routed).astype(jnp.bfloat16)
        grad_router = lax.psum(router_part, 'ep')
        grad_shared_one = lax.psum(sgrad_one, 'ep')
        grad_shared_three = lax.psum(sgrad_three, 'ep')
        grad_shared_two = lax.psum(sgrad_two, 'ep')
        return (hidden_out, grad_hidden, grad_router, wgrad_one.astype(jnp.bfloat16), wgrad_three.astype(jnp.bfloat16), wgrad_two.astype(jnp.bfloat16), grad_shared_one, grad_shared_three, grad_shared_two)

    return jax.shard_map(local_step, mesh=mesh, in_specs=(row_spec, row_spec, row_spec, copy_spec, expert_spec, expert_spec, expert_spec, copy_spec, copy_spec, copy_spec), out_specs=(row_spec, row_spec, copy_spec, expert_spec, expert_spec, expert_spec, copy_spec, copy_spec, copy_spec), check_vma=False)
```

profile of v0, /device:TPU:11, one launch (start us, length us, event | category | flops | bytes accessed | tf_op | source)
XLA Modules:
  0.0 3564.7 jit_solution(14221308177289626018)
XLA Ops:
  7.2 1.3 convert_reduce_fusion.1
  8.5 0.9 bitcast_or_fusion
  9.5 18.1 reduce-window.6
  29.2 0.7 reshape.169
  30.0 98.0 %gather_fusion.1 = s32[12288]{0:T(1024)S(1)} fusion(s32[2048,64]{0,1:T(8,128)S(1)} %fusion.44, s32[12288]{0:T(1024)S(1)} %reshape.169), kind=kCustom, calls=%fused_computation.5 | custom fusion | bytes 196608 | tf_op jit(solution)/shard_map/jit(take_along_axis)/gather | solution.py:26
  128.0 1.0 reshape.178
  129.4 0.7 compare_and_fusion
  130.4 0.8 reshape.131
  131.4 0.7 reshape.185
  132.1 45.4 %scatter_custom_fusion = s32[15360]{0:T(1024)S(1)} fusion(s32[12288]{0:T(1024)S(1)} %bitcast.160, s32[12288]{0:T(1024)S(1)} %reshape.185, s32[]{:T(128)} %constant.43.clone.1), kind=kCustom, calls=%fused_computation.101 | custom fusion | bytes 61444 | tf_op jit(solution)/shard_map/scatter | solution.py:30
  177.6 85.9 %gather_fusion.2 = bf16[15360,1280]{1,0:T(8,128)(2,1)} fusion(bf16[2048,1280]{1,0:T(8,128)(2,1)} %param.14, s32[15360]{0:T(1024)S(1)} %fusion.51), kind=kCustom, calls=%fused_computation.clone | custom fusion | bytes 78704640 | tf_op jit(solution)/shard_map/jit(_take)/gather | solution.py:99
  263.5 26.5 broadcast_select_fusion.1
  290.0 436.6 %all_to_all.20 = bf16[16,4,240,1280]{3,2,1,0:T(8,128)(2,1)} all-to-all(bf16[16,4,240,1280]{3,2,1,0:T(8,128)(2,1)} %bitcast.154), channel_id=1, replica_groups=mesh['ep'=16] {'ep'}, dimensions={0} | all-to-all | bytes 78643200 | tf_op jit(solution)/shard_map/all_to_all | solution.py:100
  726.7 51.2 %fusion.19 = f32[4,16,240,896]{3,2,1,0:T(8,128)} fusion(bf16[16,4,240,1280]{3,2,1,0:T(8,128)(2,1)} %all_to_all.20, bf16[4,1280,896]{2,1,0:T(8,128)(2,1)} %param.18), kind=kOutput, calls=%fused_computation.40 | convolution fusion | flops 35232153600 | bytes 103546880 | tf_op jit(solution)/shard_map/secd,edf->secf/dot_general | solution.py:63
  777.9 73.0 %fusion.3 = (bf16[16,4,240,896]{3,2,0,1:T(8,128)(2,1)}, f32[4,16,240,896]{3,2,1,0:T(8,128)}) fusion(f32[4,16,240,896]{3,2,1,0:T(8,128)} %fusion.19, bf16[4,1280,896]{2,1,0:T(8,128)(2,1)} %param.19, bf16[16,4,240,1280]{3,2,1,0:T(8,128)(2,1)} %all_to_all.20), kind=kOutput, calls=%fused_computation.18 | convolution fusion | flops 35314728960 | bytes 186122240 | tf_op jit(solution)/shard_map/secd,edf->secf/dot_general | solution.py:64
  850.9 49.9 %fusion.11 = bf16[16,4,240,1280]{3,2,0,1:T(8,128)(2,1)} fusion(bf16[16,4,240,896]{3,2,0,1:T(8,128)(2,1)} %get-tuple-element.72, bf16[4,896,1280]{2,1,0:T(8,128)(2,1)} %param.20), kind=kOutput, calls=%fused_computation.31 | convolution fusion | flops 35251814400 | bytes 76021760 | tf_op jit(solution)/shard_map/secf,efd->secd/dot_general | solution.py:67
  900.8 26.6 copy.92
  927.4 8.4 all-to-all-start.1
  935.9 86.0 %gather_fusion.4 = bf16[15360,1280]{1,0:T(8,128)(2,1)} fusion(bf16[2048,1280]{1,0:T(8,128)(2,1)} %param.15, s32[15360]{0:T(1024)S(1)} %copy-done.21), kind=kCustom, calls=%fused_computation.2.clone | custom fusion | bytes 78704640 | tf_op jit(solution)/shard_map/jit(_take)/gather | solution.py:107
  1022.2 1.3 reshape.210
  1023.6 1.1 copy.88
  1024.6 4.2 fusion.43
  1028.9 98.0 %gather_fusion = f32[12288]{0:T(1024)S(1)} fusion(f32[2048,64]{0,1:T(8,128)S(1)} %fusion.43, s32[12288]{0:T(1024)S(1)} %copy-done.2), kind=kCustom, calls=%fused_computation.4 | custom fusion | bytes 196608 | tf_op jit(solution)/shard_map/jit(take_along_axis)/gather | solution.py:16
  1126.9 1.0 reshape.172
  1128.3 0.6 copy-done.11
  1128.9 0.6 fusion.52
  1129.6 276.4 %all-to-all-done.1 = bf16[16,4,240,1280]{3,2,1,0:T(8,128)(2,1)} async-done(((bf16[16,4,240,1280]{3,2,1,0:T(8,128)(2,1)}), bf16[16,4,240,1280]{3,2,1,0:T(8,128)(2,1)}, u32[]{:S(2)}, u32[]{:S(2)}) %all-to-all-start.1) | async-done | bytes 39321632 | tf_op jit(solution)/shard_map/all_to_all | solution.py:102
  1406.0 282.3 %gather_fusion.3 = bf16[12288,1280]{1,0:T(8,128)(2,1)} fusion(bf16[15360,1280]{1,0:T(8,128)(2,1)} %bitcast.16, s32[12288]{0:T(1024)S(1)} %broadcast_clamp_fusion), kind=kCustom, calls=%fused_computation.1.clone | custom fusion | bytes 62963712 | tf_op jit(solution)/shard_map/jit(_take)/gather | solution.py:103
  1688.3 48.4 %reshape.213 = bf16[2048,6,1280]{2,1,0:T(8,128)(2,1)} reshape(bf16[12288,1280]{1,0:T(8,128)(2,1)} %gather_fusion.3) | data formatting | bytes 62914560 | tf_op jit(solution)/shard_map/jit(_take)/gather | solution.py:103
  1736.7 33.7 fusion.12
  1771.1 0.6 fusion.47
  1772.1 0.7 reshape.193
  1772.8 45.6 %scatter_custom_fusion.1 = f32[15360]{0:T(1024)S(1)} fusion(s32[12288]{0:T(1024)} %bitcast.161, f32[12288]{0:T(1024)S(1)} %reshape.193, f32[]{:T(128)} %constant.42.clone.1), kind=kCustom, calls=%fused_computation.99 | custom fusion | bytes 61952 | tf_op jit(solution)/shard_map/scatter | solution.py:31
  1818.4 27.4 multiply_convert_fusion
  1845.9 4.8 all-to-all-start.2
  1850.8 15.8 fusion.58
  1866.6 15.9 fusion.59
  1882.5 27.7 multiply_convert_fusion.1
  1910.2 16.1 convolution_bitcast_fusion.1
  1926.3 15.0 convolution_bitcast_fusion
  1941.4 12.9 fusion.62
  1954.8 0.7 copy-done.7
  1955.5 1.7 convolution_bitcast_fusion.2
  1957.3 433.1 %all-to-all-done.2 = bf16[16,4,240,1280]{3,2,1,0:T(8,128)(2,1)} async-done(((bf16[16,4,240,1280]{3,2,1,0:T(8,128)(2,1)}), bf16[16,4,240,1280]{3,2,1,0:T(8,128)(2,1)}, u32[]{:S(2)}, u32[]{:S(2)}) %all-to-all-start.2) | async-done | bytes 39321632 | tf_op jit(solution)/shard_map/all_to_all | solution.py:109
  2390.4 80.1 %fusion.2 = (bf16[16,4,240,896]{3,2,0,1:T(8,128)(2,1)}, bf16[16,4,240,896]{3,2,0,1:T(8,128)(2,1)}) fusion(f32[4,16,240,896]{3,2,1,0:T(8,128)} %fusion.19, f32[4,16,240,896]{3,2,1,0:T(8,128)} %get-tuple-element.73, bf16[4,896,1280]{2,1,0:T(8,128)(2,1)} %param.20, bf16[16,4,240,1280]{3,2,1,0:T(8,128)(2,1)} %all-to-all-done.2), kind=kOutput, calls=%fused_computation.16 | convolution fusion | flops 35411066880 | bytes 213647360 | tf_op jit(solution)/shard_map/secd,efd->secf/dot_general | solution.py:73
  2470.5 53.1 %fusion.36 = f32[4,16,240,1280]{3,2,1,0:T(8,128)} fusion(bf16[16,4,240,896]{3,2,0,1:T(8,128)(2,1)} %get-tuple-element.68, bf16[4,1280,896]{2,1,0:T(8,128)(2,1)} %param.18), kind=kOutput, calls=%fused_computation.60 | convolution fusion | flops 35232153600 | bytes 115343360 | tf_op jit(solution)/shard_map/secf,edf->secd/dot_general | solution.py:79
  2523.6 61.5 %fusion.10 = bf16[16,4,240,1280]{3,2,0,1:T(8,128)(2,1)} fusion(f32[4,16,240,1280]{3,2,1,0:T(8,128)} %fusion.36, bf16[16,4,240,896]{3,2,0,1:T(8,128)(2,1)} %get-tuple-element.67, bf16[4,1280,896]{2,1,0:T(8,128)(2,1)} %param.19), kind=kOutput, calls=%fused_computation.30 | convolution fusion | flops 35271475200 | bytes 154664960 | tf_op jit(solution)/shard_map/secf,edf->secd/dot_general | solution.py:79
  2585.1 26.6 copy.97
  2611.7 6.6 all-to-all-start.3
  2618.4 15.8 fusion.60
  2634.2 12.3 fusion.61
  2646.4 10.8 copy.102
  2657.2 10.8 copy.103
  2668.0 45.2 %bitcast_convert_fusion = bf16[4,896,1280]{2,1,0:T(8,128)(2,1)} fusion(bf16[16,4,240,896]{3,2,0,1:T(8,128)(2,1)} %get-tuple-element.72, bf16[16,4,240,1280]{3,2,1,0:T(8,128)(2,1)} %all-to-all-done.2), kind=kOutput, calls=%fused_computation.47 | convolution fusion | flops 35236741120 | bytes 76021760 | tf_op jit(solution)/shard_map/secf,secd->efd/dot_general | solution.py:76
  2713.2 49.7 %bitcast_convert_fusion.2 = bf16[4,1280,896]{2,1,0:T(8,128)(2,1)} fusion(bf16[16,4,240,1280]{3,2,1,0:T(8,128)(2,1)} %all_to_all.20, bf16[16,4,240,896]{3,2,0,1:T(8,128)(2,1)} %get-tuple-element.68), kind=kOutput, calls=%fused_computation.49 | convolution fusion | flops 35236741120 | bytes 76021760 | tf_op jit(solution)/shard_map/secd,secf->edf/dot_general | solution.py:77
  2762.9 49.8 %bitcast_convert_fusion.1 = bf16[4,1280,896]{2,1,0:T(8,128)(2,1)} fusion(bf16[16,4,240,1280]{3,2,1,0:T(8,128)(2,1)} %all_to_all.20, bf16[16,4,240,896]{3,2,0,1:T(8,128)(2,1)} %get-tuple-element.67), kind=kOutput, calls=%fused_computation.48 | convolution fusion | flops 35236741120 | bytes 76021760 | tf_op jit(solution)/shard_map/secd,secf->edf/dot_general | solution.py:78
  2812.6 289.5 %all-to-all-done.3 = bf16[16,4,240,1280]{3,2,1,0:T(8,128)(2,1)} async-done(((bf16[16,4,240,1280]{3,2,1,0:T(8,128)(2,1)}), bf16[16,4,240,1280]{3,2,1,0:T(8,128)(2,1)}, u32[]{:S(2)}, u32[]{:S(2)}) %all-to-all-start.3) | async-done | bytes 39321632 | tf_op jit(solution)/shard_map/all_to_all | solution.py:111
  3102.1 283.3 %gather_fusion.5 = bf16[12288,1280]{1,0:T(8,128)(2,1)} fusion(bf16[15360,1280]{1,0:T(8,128)(2,1)} %bitcast.25, s32[12288]{0:T(1024)S(1)} %copy-done.4), kind=kCustom, calls=%fused_computation.3.clone | custom fusion | bytes 62963712 | tf_op jit(solution)/shard_map/jit(_take)/gather | solution.py:112
  3385.4 48.5 %reshape.219 = bf16[2048,6,1280]{2,1,0:T(8,128)(2,1)} reshape(bf16[12288,1280]{1,0:T(8,128)(2,1)} %gather_fusion.5) | data formatting | bytes 62914560 | tf_op jit(solution)/shard_map/jit(_take)/gather | solution.py:112
  3434.0 84.2 %convert_reduce_fusion = (f32[2048,1280]{1,0:T(8,128)}, f32[2048,1280]{1,0:T(8,128)}) fusion(bf16[2048,6,1280]{2,1,0:T(8,128)(2,1)} %reshape.219, pred[2048,6]{1,0:T(8,128)(4,1)S(1)} %copy-done.10, bf16[2048,6,1280]{2,1,0:T(8,128)(2,1)} %reshape.213, f32[2048,6]{1,0:T(8,128)S(1)} %copy-done.6), kind=kLoop, calls=%fused_computation.8 | loop fusion | flops 104857600 | bytes 83947520 | tf_op jit(solution)/shard_map/reduce_sum | solution.py:112
  3518.2 15.4 add_convert_fusion.1
  3533.6 15.2 add_convert_fusion
  3548.7 0.7 copy.142
  3549.5 7.8 copy.143
  (119 shorter events, 4.9 us)
Async XLA Ops:
  7.2 1017.5 %copy-start = (bf16[1280,64]{0,1:T(8,128)(2,1)S(1)}, bf16[1280,64]{0,1:T(8,128)(2,1)}, u32[]{:S(2)}) copy-start(bf16[1280,64]{0,1:T(8,128)(2,1)} %param.17) | copy-start | bytes 491524
  29.9 98.1 %copy-start.1 = (s32[12288]{0:T(1024)}, s32[12288]{0:T(1024)S(1)}, u32[]{:S(2)}) copy-start(s32[12288]{0:T(1024)S(1)} %reshape.169) | copy-start | bytes 147460
  29.9 99.4 %copy-start.14 = (s32[2048,6]{0,1:T(8,128)S(1)}, s32[2048,6]{0,1:T(8,128)}, u32[]{:S(2)}) copy-start(s32[2048,6]{0,1:T(8,128)} %param.16) | copy-start | bytes 147460
  130.1 133.5 %copy-start.18 = (s32[2048,6]{0,1:T(8,128)}, s32[2048,6]{0,1:T(8,128)S(1)}, u32[]{:S(2)}) copy-start(s32[2048,6]{0,1:T(8,128)S(1)} %get-tuple-element.65) | copy-start | bytes 147460
  131.3 132.2 %copy-start.32 = (s32[12288,1]{0,1:T(1,128)}, s32[12288,1]{0,1:T(1,128)S(1)}, u32[]{:S(2)}) copy-start(s32[12288,1]{0,1:T(1,128)S(1)} %compare_select_fusion) | copy-start | bytes 147460
  177.6 86.0 %copy-start.20 = (s32[15360]{0:T(1024)}, s32[15360]{0:T(1024)S(1)}, u32[]{:S(2)}) copy-start(s32[15360]{0:T(1024)S(1)} %fusion.51) | copy-start | bytes 184324
  177.6 85.9 %copy-start.27 = (pred[15360]{0:T(1024)(128)(4,1)}, pred[15360]{0:T(1024)(128)(4,1)S(1)}, u32[]{:S(2)}) copy-start(pred[15360]{0:T(1024)(128)(4,1)S(1)} %compare_and_fusion.2) | copy-start | bytes 46084
  927.4 8.4 copy-start.21
  927.4 478.5 %all-to-all-start.1 = ((bf16[16,4,240,1280]{3,2,1,0:T(8,128)(2,1)}), bf16[16,4,240,1280]{3,2,1,0:T(8,128)(2,1)}, u32[]{:S(2)}, u32[]{:S(2)}) async-start(bf16[16,4,240,1280]{3,2,1,0:T(8,128)(2,1)} %copy.92), calls=%async_computation.1 | async-start | bytes 78643200 | tf_op jit(solution)/shard_map/all_to_all | solution.py:102
  935.8 86.0 %copy-start.19 = (s32[2048,6]{0,1:T(8,128)S(1)}, s32[2048,6]{0,1:T(8,128)}, u32[]{:S(2)}) copy-start(s32[2048,6]{0,1:T(8,128)} %copy-done.18) | copy-start | bytes 147460
  935.8 87.7 %copy-start.31 = (pred[2048,6]{0,1:T(8,128)(4,1)S(1)}, pred[2048,6]{0,1:T(8,128)(4,1)}, u32[]{:S(2)}) copy-start(pred[2048,6]{0,1:T(8,128)(4,1)} %get-tuple-element.64) | copy-start | bytes 36868
  1021.8 7.0 copy-start.2
  1028.9 100.1 %copy-start.23 = (pred[2048,6]{0,1:T(8,128)(4,1)S(1)}, pred[2048,6]{0,1:T(8,128)(4,1)}, u32[]{:S(2)}) copy-start(pred[2048,6]{0,1:T(8,128)(4,1)} %get-tuple-element.66) | copy-start | bytes 36868
  1028.9 100.7 %copy-start.26 = (s32[12288]{0:T(1024)S(1)}, s32[12288]{0:T(1024)}, u32[]{:S(2)}) copy-start(s32[12288]{0:T(1024)} %reshape.210) | copy-start | bytes 147460
  1128.3 0.6 copy-start.11
  1129.6 558.7 %copy-start.3 = (s32[12288]{0:T(1024)}, s32[12288]{0:T(1024)S(1)}, u32[]{:S(2)}) copy-start(s32[12288]{0:T(1024)S(1)} %broadcast_clamp_fusion) | copy-start | bytes 147460
  1688.3 48.4 %copy-start.9 = (pred[2048,6]{1,0:T(8,128)(4,1)S(1)}, pred[2048,6]{1,0:T(8,128)(4,1)}, u32[]{:S(2)}) copy-start(pred[2048,6]{1,0:T(8,128)(4,1)} %copy.88) | copy-start | bytes 36868
  1736.7 34.3 copy-start.12
  1736.7 34.3 copy-start.24
  1736.7 34.3 copy-start.29
  1736.7 81.7 %copy-start.28 = (pred[15360]{0:T(1024)(128)(4,1)S(1)}, pred[15360]{0:T(1024)(128)(4,1)}, u32[]{:S(2)}) copy-start(pred[15360]{0:T(1024)(128)(4,1)} %copy-done.27) | copy-start | bytes 46084
  1771.1 0.6 copy-start.16
  1772.1 73.8 %copy-start.5 = (f32[2048,6]{1,0:T(8,128)}, f32[2048,6]{1,0:T(8,128)S(1)}, u32[]{:S(2)}) copy-start(f32[2048,6]{1,0:T(8,128)S(1)} %copy.84) | copy-start | bytes 147460
  1845.9 544.6 %all-to-all-start.2 = ((bf16[16,4,240,1280]{3,2,1,0:T(8,128)(2,1)}), bf16[16,4,240,1280]{3,2,1,0:T(8,128)(2,1)}, u32[]{:S(2)}, u32[]{:S(2)}) async-start(bf16[16,4,240,1280]{3,2,1,0:T(8,128)(2,1)} %bitcast.153), calls=%async_computation.2 | async-start | bytes 78643200 | tf_op jit(solution)/shard_map/all_to_all | solution.py:109
  1850.7 795.7 %all-reduce.3.cloned.1.call-start = ((), (), s32[]{:S(2)}) async-start(), calls=%async_computation.4 | async-start | bytes 55705600 | tf_op jit(solution)/shard_map/psum | solution.py:119
  1910.2 16.1 copy-start.36
  1910.2 31.1 slice-start.4
  1910.2 31.1 slice-start.6
  1926.3 15.0 slice-start.5
  1926.3 15.0 slice-start.7
  1926.3 29.3 slice-start
  1941.3 13.0 copy-start.30
  1941.3 13.0 copy-start.33
  1941.4 13.0 copy-start.13
  1941.4 13.0 copy-start.17
  1941.4 13.0 copy-start.25
  1941.4 13.0 copy-start.15
  1941.4 14.1 slice-start.1
  1954.8 0.7 copy-start.7
  2611.7 490.4 %all-to-all-start.3 = ((bf16[16,4,240,1280]{3,2,1,0:T(8,128)(2,1)}), bf16[16,4,240,1280]{3,2,1,0:T(8,128)(2,1)}, u32[]{:S(2)}, u32[]{:S(2)}) async-start(bf16[16,4,240,1280]{3,2,1,0:T(8,128)(2,1)} %copy.97), calls=%async_computation.3 | async-start | bytes 78643200 | tf_op jit(solution)/shard_map/all_to_all | solution.py:111
  2618.4 15.8 copy-start.34
  2618.4 15.8 copy-start.37
  2762.9 339.2 %copy-start.4 = (s32[12288]{0:T(1024)S(1)}, s32[12288]{0:T(1024)}, u32[]{:S(2)}) copy-start(s32[12288]{0:T(1024)} %copy-done.3) | copy-start | bytes 147460
  3385.4 48.5 %copy-start.6 = (f32[2048,6]{1,0:T(8,128)S(1)}, f32[2048,6]{1,0:T(8,128)}, u32[]{:S(2)}) copy-start(f32[2048,6]{1,0:T(8,128)} %copy-done.5) | copy-start | bytes 147460
  3385.4 48.5 %copy-start.10 = (pred[2048,6]{1,0:T(8,128)(4,1)S(1)}, pred[2048,6]{1,0:T(8,128)(4,1)}, u32[]{:S(2)}) copy-start(pred[2048,6]{1,0:T(8,128)(4,1)} %copy.88) | copy-start | bytes 36868
  3385.4 132.8 %slice-start.2 = ((s8[5242880]{0:T(1024)(128)(4,1)}), s8[1048576]{0:T(1024)(128)(4,1)S(1)}, s32[]{:S(2)}) async-start(s8[5242880]{0:T(1024)(128)(4,1)} %bitcast.148), calls=%async_computation.7 | async-start | bytes 2097152
  3434.0 84.2 %slice-start.3 = ((s8[5242880]{0:T(1024)(128)(4,1)}), s8[4194304]{0:T(1024)(128)(4,1)S(1)}, s32[]{:S(2)}) async-start(s8[5242880]{0:T(1024)(128)(4,1)} %bitcast.148), calls=%async_computation.8 | async-start | bytes 8388608
  3434.0 84.2 %copy-start.35 = (bf16[1792,1280]{1,0:T(8,128)(2,1)S(1)}, bf16[1792,1280]{1,0:T(8,128)(2,1)}, u32[]{:S(2)}) copy-start(bf16[1792,1280]{1,0:T(8,128)(2,1)} %param.23) | copy-start | bytes 13762564
  3518.2 15.4 copy-start.8
  3533.6 15.2 copy-start.22
Sparse Core Ops, SparseCore 0:
  1957.4 628.5 all-reduce.2
where the time goes:
time: 3580 us; the launch traced here: 3560 us
  local copies, waits for them, and re-layouts  1220 us (34%)
  waiting for transfers between devices  999 us (28%)
  matrix products  715 us (20%)
  blocking collectives  437 us (12%)
  other arithmetic  162 us (5%)
    all_to_all x1, blocking collectives, local_step(): recv_rows = lax.all_to_all(send_rows, 'ep', 0, 0)  437 us
    all_to_all x1, waiting for transfers between devices, local_step(): grad_recv = lax.all_to_all(grad_send, 'ep', 0, 0)  433 us
    gather x2, local copies, waits for them, and re-layouts, local_step(): jnp.take(dx_back, slot_ids, axis=0, mode='fill', fill_value=0)  332 us
    gather x2, local copies, waits for them, and re-layouts, local_step(): gathered = jnp.take(back_rows, slot_ids, axis=0, mode='fill', fill_value=0)  331 us
    all_to_all x1, waiting for transfers between devices, local_step(): dx_back = lax.all_to_all(dx_rows, 'ep', 0, 0).reshape(flat_shape)  289 us
    all_to_all x1, waiting for transfers between devices, local_step(): back_rows = lax.all_to_all(expert_out, 'ep', 0, 0).reshape(flat_shape)  276 us
    gather x5, local copies, waits for them, and re-layouts, router_weights(): picked = jnp.take_along_axis(jax.nn.sigmoid(logits), routes, axis=1)  100 us
    gather x3, local copies, waits for them, and re-layouts, slot_tables(): position = jnp.take_along_axis(before, routes, axis=1)  99.4 us
  transfers between devices with their start and end apart: 4, of which 3 were waited for; matrix products, arithmetic and copies ran while one was open for 20% of the time, Pallas kernels for 0%

commit v1 on v0

v1 whole, which is shorter than its diff:
```python
import functools

import jax
import jax.numpy as jnp
from jax import lax
from jax.experimental import pallas as pl
from jax.experimental.pallas import tpu as pltpu
from jax.sharding import PartitionSpec as P


ROUTE_SCALE = 2.5
STRIDE = 256
VMEM_LIMIT = 60 * 1024 * 1024


def silu_parts(pre_act):
    sig_val = jax.nn.sigmoid(pre_act)
    return pre_act * sig_val, sig_val * (1.0 + pre_act * (1.0 - sig_val))


def route_tables(hidden, routes, w_router, capacity):
    tok_count = hidden.shape[0]
    num_experts = w_router.shape[1]
    logits = jnp.dot(hidden, w_router, preferred_element_type=jnp.float32)
    scores = jax.nn.sigmoid(logits)
    expert_ids = jnp.arange(num_experts, dtype=jnp.int32)
    chosen = routes[:, 0:1] == expert_ids
    for j in range(1, routes.shape[1]):
        chosen = chosen | (routes[:, j : j + 1] == expert_ids)
    picked = jnp.where(chosen, scores, 0.0)
    pick_sum = jnp.sum(picked, axis=1, keepdims=True)
    weights = ROUTE_SCALE * picked / pick_sum
    hit = chosen.astype(jnp.bfloat16)
    rows = lax.broadcasted_iota(jnp.int32, (tok_count, tok_count), 0)
    cols = lax.broadcasted_iota(jnp.int32, (tok_count, tok_count), 1)
    earlier = (cols < rows).astype(jnp.bfloat16)
    before = jnp.dot(earlier, hit, preferred_element_type=jnp.float32)
    kept = chosen & (before < capacity)
    position = jnp.where(kept, before, -1.0)
    return scores, chosen, pick_sum, weights, position


def select_kernel(pos_ref, rows_ref, out_ref, sel_ref):
    tok_count, d_model = rows_ref.shape
    local_experts, capacity, _ = out_ref.shape
    slot_iota = lax.broadcasted_iota(jnp.int32, (capacity, tok_count), 0).astype(jnp.float32)
    for el in range(local_experts):
        hit = slot_iota == pos_ref[0, el : el + 1, :]
        sel_ref[el * capacity : (el + 1) * capacity, :] = jnp.where(hit, 1.0, 0.0).astype(jnp.bfloat16)
    width = 256
    for n in range(d_model // width):
        w = slice(n * width, (n + 1) * width)
        part = jnp.dot(sel_ref[...], rows_ref[:, w], preferred_element_type=jnp.float32).astype(jnp.bfloat16)
        for el in range(local_experts):
            out_ref[el, :, w] = part[el * capacity : (el + 1) * capacity, :]


def select_rows(all_rows, plan, capacity):
    group_size, double, tok_count = plan.shape
    local_experts = double // 2
    d_model = all_rows.shape[1]
    slots = local_experts * capacity
    return pl.pallas_call(
        select_kernel,
        grid=(group_size,),
        in_specs=[
            pl.BlockSpec((1, double, tok_count), lambda g: (g, 0, 0)),
            pl.BlockSpec((tok_count, d_model), lambda g: (g, 0)),
        ],
        out_specs=pl.BlockSpec((local_experts, capacity, d_model), lambda g: (0, g, 0)),
        out_shape=jax.ShapeDtypeStruct((local_experts, group_size * capacity, d_model), jnp.bfloat16),
        scratch_shapes=[pltpu.VMEM((slots, tok_count), jnp.bfloat16)],
        compiler_params=pltpu.CompilerParams(vmem_limit_bytes=VMEM_LIMIT),
        cost_estimate=pl.CostEstimate(flops=2 * group_size * slots * tok_count * d_model, bytes_accessed=2 * group_size * (slots + tok_count) * d_model, transcendentals=0),
    )(plan, all_rows)


def select_grad_kernel(pos_ref, rows_ref, outs_ref, q_ref, dot_ref, sel_ref):
    tok_count, d_model = rows_ref.shape
    local_experts, capacity, _ = q_ref.shape
    slot_iota = lax.broadcasted_iota(jnp.int32, (capacity, tok_count), 0).astype(jnp.float32)
    w_cols = []
    for el in range(local_experts):
        hit = slot_iota == pos_ref[0, el : el + 1, :]
        sel_ref[el * capacity : (el + 1) * capacity, :] = jnp.where(hit, 1.0, 0.0).astype(jnp.bfloat16)
        w_row = pos_ref[0, local_experts + el : local_experts + el + 1, :]
        w_cols.append(jnp.sum(jnp.where(hit, w_row, 0.0), axis=1, keepdims=True))
    dots = [jnp.zeros((capacity, 1), jnp.float32) for _ in range(local_experts)]
    width = 256
    for n in range(d_model // width):
        w = slice(n * width, (n + 1) * width)
        part = jnp.dot(sel_ref[...], rows_ref[:, w], preferred_element_type=jnp.float32)
        for el in range(local_experts):
            grad = part[el * capacity : (el + 1) * capacity, :]
            q_ref[el, :, w] = (w_cols[el] * grad).astype(jnp.bfloat16)
            dots[el] = dots[el] + jnp.sum(grad * outs_ref[0, el, :, w].astype(jnp.float32), axis=1, keepdims=True)
    for el in range(local_experts):
        dot_ref[0, el * capacity : (el + 1) * capacity, :] = jnp.broadcast_to(dots[el], (capacity, 128))


def select_grads(all_grads, plan, expert_outs, capacity):
    group_size, double, tok_count = plan.shape
    local_experts = double // 2
    d_model = all_grads.shape[1]
    slots = local_experts * capacity
    q_rows, slot_dots = pl.pallas_call(
        select_grad_kernel,
        grid=(group_size,),
        in_specs=[
            pl.BlockSpec((1, double, tok_count), lambda g: (g, 0, 0)),
            pl.BlockSpec((tok_count, d_model), lambda g: (g, 0)),
            pl.BlockSpec((1, local_experts, capacity, d_model), lambda g: (g, 0, 0, 0)),
        ],
        out_specs=[pl.BlockSpec((local_experts, capacity, d_model), lambda g: (0, g, 0)), pl.BlockSpec((1, slots, 128), lambda g: (g, 0, 0))],
        out_shape=[jax.ShapeDtypeStruct((local_experts, group_size * capacity, d_model), jnp.bfloat16), jax.ShapeDtypeStruct((group_size, slots, 128), jnp.float32)],
        scratch_shapes=[pltpu.VMEM((slots, tok_count), jnp.bfloat16)],
        compiler_params=pltpu.CompilerParams(vmem_limit_bytes=VMEM_LIMIT),
        cost_estimate=pl.CostEstimate(flops=2 * group_size * slots * tok_count * d_model, bytes_accessed=2 * group_size * (3 * slots + tok_count) * d_model, transcendentals=0),
    )(plan, all_grads, expert_outs)
    return q_rows, slot_dots[:, :, 0]


def forward_kernel(x_ref, one_ref, three_ref, two_ref, pre_one_ref, pre_three_ref, mid_ref, out_ref):
    groups, _, capacity, d_model = out_ref.shape
    pre_one_ref[0] = jnp.dot(x_ref[0], one_ref[0], preferred_element_type=jnp.float32)
    pre_three_ref[0] = jnp.dot(x_ref[0], three_ref[0], preferred_element_type=jnp.float32)

    def middle(r, carry):
        span = pl.ds(pl.multiple_of(r * 48, 48), 48)
        pre_one = pre_one_ref[0, span, :]
        mid_ref[0, span, :] = (pre_one * jax.nn.sigmoid(pre_one) * pre_three_ref[0, span, :]).astype(jnp.bfloat16)
        return carry

    lax.fori_loop(0, groups * capacity // 48, middle, 0)
    width = 256
    for n in range(d_model // width):
        w = slice(n * width, (n + 1) * width)
        part = jnp.dot(mid_ref[0], two_ref[0, :, w], preferred_element_type=jnp.float32).astype(jnp.bfloat16)
        for g in range(groups):
            out_ref[g, 0, :, w] = part[g * capacity : (g + 1) * capacity, :]


def expert_forward(rows, w_one, w_three, w_two, group_size, groups=4):
    local_experts, total, d_model = rows.shape
    d_ff = w_one.shape[2]
    capacity = total // group_size
    tile = groups * capacity
    rows_spec = pl.BlockSpec((1, tile, d_model), lambda e, m: (e, m, 0))
    mid_spec = pl.BlockSpec((1, tile, d_ff), lambda e, m: (e, m, 0))
    up_spec = pl.BlockSpec((1, d_model, d_ff), lambda e, m: (e, 0, 0))
    down_spec = pl.BlockSpec((1, d_ff, d_model), lambda e, m: (e, 0, 0))
    return pl.pallas_call(
        forward_kernel,
        grid=(local_experts, group_size // groups),
        in_specs=[rows_spec, up_spec, up_spec, down_spec],
        out_specs=[mid_spec, mid_spec, mid_spec, pl.BlockSpec((groups, 1, capacity, d_model), lambda e, m: (m, e, 0, 0))],
        out_shape=[
            jax.ShapeDtypeStruct((local_experts, total, d_ff), jnp.float32),
            jax.ShapeDtypeStruct((local_experts, total, d_ff), jnp.float32),
            jax.ShapeDtypeStruct((local_experts, total, d_ff), jnp.bfloat16),
            jax.ShapeDtypeStruct((group_size, local_experts, capacity, d_model), jnp.bfloat16),
        ],
        compiler_params=pltpu.CompilerParams(vmem_limit_bytes=VMEM_LIMIT),
        cost_estimate=pl.CostEstimate(flops=6 * local_experts * total * d_model * d_ff, bytes_accessed=local_experts * total * (4 * d_model + 10 * d_ff), transcendentals=local_experts * total * d_ff),
    )(rows, w_one, w_three, w_two)


def backward_kernel(q_ref, pre_one_ref, pre_three_ref, one_ref, three_ref, two_ref, u_ref, v_ref, dx_ref, mid_ref):
    groups, _, capacity, d_model = dx_ref.shape
    flip = (((1,), (1,)), ((), ()))
    mid_ref[...] = lax.dot_general(q_ref[0], two_ref[0], flip, preferred_element_type=jnp.float32)

    def middle(r, carry):
        span = pl.ds(pl.multiple_of(r * 48, 48), 48)
        pre_one = pre_one_ref[0, span, :]
        grad_mid = mid_ref[span, :]
        act_one, dact_one = silu_parts(pre_one)
        u_ref[0, span, :] = (grad_mid * pre_three_ref[0, span, :] * dact_one).astype(jnp.bfloat16)
        v_ref[0, span, :] = (grad_mid * act_one).astype(jnp.bfloat16)
        return carry

    lax.fori_loop(0, groups * capacity // 48, middle, 0)
    width = 256
    for n in range(d_model // width):
        w = slice(n * width, (n + 1) * width)
        part = lax.dot_general(u_ref[0], one_ref[0, w, :], flip, preferred_element_type=jnp.float32)
        part += lax.dot_general(v_ref[0], three_ref[0, w, :], flip, preferred_element_type=jnp.float32)
        part = part.astype(jnp.bfloat16)
        for g in range(groups):
            dx_ref[g, 0, :, w] = part[g * capacity : (g + 1) * capacity, :]


def expert_backward(q_rows, pre_one, pre_three, w_one, w_three, w_two, group_size, first, count, groups=4):
    _, total, d_model = q_rows.shape
    d_ff = w_one.shape[2]
    capacity = total // group_size
    tile = groups * capacity
    rows_spec = pl.BlockSpec((1, tile, d_model), lambda e, m: (first + e, m, 0))
    mid_spec = pl.BlockSpec((1, tile, d_ff), lambda e, m: (first + e, m, 0))
    new_spec = pl.BlockSpec((1, tile, d_ff), lambda e, m: (e, m, 0))
    up_spec = pl.BlockSpec((1, d_model, d_ff), lambda e, m: (first + e, 0, 0))
    down_spec = pl.BlockSpec((1, d_ff, d_model), lambda e, m: (first + e, 0, 0))
    return pl.pallas_call(
        backward_kernel,
        grid=(count, group_size // groups),
        in_specs=[rows_spec, mid_spec, mid_spec, up_spec, up_spec, down_spec],
        out_specs=[new_spec, new_spec, pl.BlockSpec((groups, 1, capacity, d_model), lambda e, m: (m, e, 0, 0))],
        out_shape=[
            jax.ShapeDtypeStruct((count, total, d_ff), jnp.bfloat16),
            jax.ShapeDtypeStruct((count, total, d_ff), jnp.bfloat16),
            jax.ShapeDtypeStruct((group_size, count, capacity, d_model), jnp.bfloat16),
        ],
        scratch_shapes=[pltpu.VMEM((tile, d_ff), jnp.float32)],
        compiler_params=pltpu.CompilerParams(vmem_limit_bytes=VMEM_LIMIT),
        cost_estimate=pl.CostEstimate(flops=6 * count * total * d_model * d_ff, bytes_accessed=count * total * (4 * d_model + 12 * d_ff), transcendentals=count * total * d_ff),
    )(q_rows, pre_one, pre_three, w_one, w_three, w_two)


def combine_kernel(weighted, first, *refs):
    if weighted:
        cols_ref, dots_ref, rows_ref, acc_ref, tok_dot_ref, stack_ref, t_refs = refs[0], refs[1], refs[2], refs[3], refs[4], refs[5], refs[6:]
    else:
        cols_ref, rows_ref, acc_ref, stack_ref, t_refs = refs[0], refs[1], refs[2], refs[3], refs[4:]
    step = pl.program_id(0)
    segs, capacity, d_model = rows_ref.shape
    tok_count = acc_ref.shape[0]
    tile = t_refs[0].shape[0]

    @pl.when(step == 0)
    def _():
        acc_ref[...] = jnp.zeros_like(acc_ref)
        stack_ref[...] = jnp.zeros_like(stack_ref)
        if weighted:
            tok_dot_ref[...] = jnp.zeros_like(tok_dot_ref)

    for s in range(segs):
        stack_ref[s * STRIDE : s * STRIDE + capacity, :] = rows_ref[s]
    lane_iota = lax.broadcasted_iota(jnp.int32, (tile, STRIDE), 1).astype(jnp.float32)
    if weighted:
        expert_iota = lax.broadcasted_iota(jnp.int32, (tile, tok_dot_ref.shape[1]), 1)

    def body(m, carry):
        span = pl.ds(pl.multiple_of(m * tile, tile), tile)
        cols = cols_ref[0, span, :]
        if weighted:
            dots = jnp.zeros((tile, tok_dot_ref.shape[1]), jnp.float32)
        for s in range(segs):
            hit = lane_iota == cols[:, s : s + 1]
            slots = slice(s * STRIDE, (s + 1) * STRIDE)
            if weighted:
                for k, t_ref in enumerate(t_refs):
                    c = (k + 1) * segs + s
                    t_ref[:, slots] = jnp.where(hit, cols[:, c : c + 1], 0.0).astype(jnp.bfloat16)
                col = jnp.sum(jnp.where(hit, dots_ref[0, s : s + 1, :], 0.0), axis=1, keepdims=True)
                dots = dots + jnp.where(expert_iota == (first + step) * segs + s, col, 0.0)
            else:
                t_refs[0][:, slots] = jnp.where(hit, 1.0, 0.0).astype(jnp.bfloat16)
        if weighted:
            tok_dot_ref[span, :] += dots
        width = 256
        for n in range(d_model // width):
            w = slice(n * width, (n + 1) * width)
            part = jnp.dot(t_refs[0][...], stack_ref[:, w], preferred_element_type=jnp.float32)
            for t_ref in t_refs[1:]:
                part += jnp.dot(t_ref[...], stack_ref[:, w], preferred_element_type=jnp.float32)
            acc_ref[span, w] += part
        return carry

    lax.fori_loop(0, tok_count // tile, body, 0)


def combine(cols, rows, first, steps, dots=None, segs=4, tile=512):
    _, tok_count, width = cols.shape
    _, capacity, d_model = rows.shape
    weighted = dots is not None
    terms = 3 if weighted else 1
    in_specs = [pl.BlockSpec((1, tok_count, width), lambda d: (first + d, 0, 0))]
    args = [cols]
    out_specs = [pl.BlockSpec((tok_count, d_model), lambda d: (0, 0))]
    out_shape = [jax.ShapeDtypeStruct((tok_count, d_model), jnp.float32)]
    if weighted:
        in_specs.append(pl.BlockSpec((1, segs, STRIDE), lambda d: (first + d, 0, 0)))
        args.append(dots)
        out_specs.append(pl.BlockSpec((tok_count, 128), lambda d: (0, 0)))
        out_shape.append(jax.ShapeDtypeStruct((tok_count, 128), jnp.float32))
    in_specs.append(pl.BlockSpec((segs, capacity, d_model), lambda d: (first + d, 0, 0)))
    args.append(rows)
    return pl.pallas_call(
        functools.partial(combine_kernel, weighted, first),
        grid=(steps,),
        in_specs=in_specs,
        out_specs=out_specs,
        out_shape=out_shape,
        scratch_shapes=[pltpu.VMEM((segs * STRIDE, d_model), jnp.bfloat16)] + [pltpu.VMEM((tile, segs * STRIDE), jnp.bfloat16)] * terms,
        compiler_params=pltpu.CompilerParams(vmem_limit_bytes=VMEM_LIMIT),
        cost_estimate=pl.CostEstimate(flops=2 * terms * steps * segs * STRIDE * tok_count * d_model, bytes_accessed=2 * steps * segs * capacity * d_model + 4 * tok_count * d_model, transcendentals=0),
    )(*args)


def shared_forward(hidden, shared_one, shared_three, shared_two):
    pre_one = jnp.dot(hidden, shared_one, preferred_element_type=jnp.float32)
    pre_three = jnp.dot(hidden, shared_three, preferred_element_type=jnp.float32)
    act_one, dact_one = silu_parts(pre_one)
    mid_act = (act_one * pre_three).astype(jnp.bfloat16)
    return jnp.dot(mid_act, shared_two, preferred_element_type=jnp.float32), (pre_three, act_one, dact_one, mid_act)


def shared_backward(hidden, grad_out, saved_acts, shared_one, shared_three, shared_two):
    pre_three, act_one, dact_one, mid_act = saved_acts
    grad_mid = jnp.einsum('td,fd->tf', grad_out, shared_two, preferred_element_type=jnp.float32)
    grad_one = (grad_mid * pre_three * dact_one).astype(jnp.bfloat16)
    grad_three = (grad_mid * act_one).astype(jnp.bfloat16)
    wgrad_one = jnp.einsum('td,tf->df', hidden, grad_one, preferred_element_type=jnp.float32)
    wgrad_three = jnp.einsum('td,tf->df', hidden, grad_three, preferred_element_type=jnp.float32)
    wgrad_two = jnp.einsum('tf,td->fd', mid_act, grad_out, preferred_element_type=jnp.float32)
    dx_part = jnp.einsum('tf,df->td', grad_one, shared_one, preferred_element_type=jnp.float32) + jnp.einsum('tf,df->td', grad_three, shared_three, preferred_element_type=jnp.float32)
    return dx_part, wgrad_one, wgrad_three, wgrad_two


def solution(mesh):
    group_size = mesh.shape['ep']
    row_spec = P('ep', None)
    expert_spec = P('ep', None, None)
    copy_spec = P()

    def layer(hidden, grad_out, routes, w_router, w_one, w_three, w_two, shared_one, shared_three, shared_two):
        tok_count, d_model = hidden.shape
        top_k = routes.shape[1]
        num_experts = w_router.shape[1]
        local_experts = w_one.shape[0]
        capacity = (5 * tok_count * top_k + 4 * num_experts - 1) // (4 * num_experts)
        all_hidden = lax.all_gather(hidden, 'ep', axis=0, tiled=True)
        all_grads = lax.all_gather(grad_out, 'ep', axis=0, tiled=True)

        scores, chosen, pick_sum, weights, position = route_tables(hidden, routes, w_router, capacity)
        pos_t = position.T.reshape(group_size, local_experts, tok_count)
        w_t = weights.T.reshape(group_size, local_experts, tok_count)
        plan = lax.all_to_all(jnp.concatenate([pos_t, w_t], axis=1), 'ep', 0, 0)
        w_hi = lax.reduce_precision(weights, 8, 7)
        w_mid = lax.reduce_precision(weights - w_hi, 8, 7)
        w_low = weights - w_hi - w_mid
        segs = local_experts

        def to_cols(table):
            return table.reshape(tok_count, group_size, segs).transpose(1, 0, 2)

        def part_cols(table, lo, hi):
            part = table.reshape(tok_count, group_size, local_experts)[:, :, lo:hi]
            return part.reshape(tok_count, -1, segs).transpose(1, 0, 2)

        def to_tokens(rows):
            rows = rows.reshape(group_size, -1, d_model)
            return lax.all_to_all(rows, 'ep', 0, 0).reshape(-1, capacity, d_model)

        shared_out, shared_saved = shared_forward(hidden, shared_one, shared_three, shared_two)
        shared_dx, sgrad_one, sgrad_three, sgrad_two = shared_backward(hidden, grad_out, shared_saved, shared_one, shared_three, shared_two)
        grad_shared_one, grad_shared_three, grad_shared_two = lax.psum((sgrad_one, sgrad_three, sgrad_two), 'ep')
        recv_rows = select_rows(all_hidden, plan, capacity)
        pre_one, pre_three, mid_act, expert_out = expert_forward(recv_rows, w_one, w_three, w_two, group_size)
        back_out = to_tokens(expert_out)
        grad_recv, slot_dots = select_grads(all_grads, plan, expert_out, capacity)
        dot_back = lax.all_to_all(slot_dots, 'ep', 0, 0).reshape(group_size, local_experts, capacity)
        dot_back = jnp.pad(dot_back, ((0, 0), (0, 0), (0, STRIDE - capacity)))
        backward = lambda lo, hi: expert_backward(grad_recv, pre_one, pre_three, w_one, w_three, w_two, group_size, lo, hi - lo)
        cut = local_experts - 1
        u_a, v_a, dx_a = backward(0, cut)
        u_b, v_b, dx_b = backward(cut, local_experts)
        dx_back_a = to_tokens(dx_a)
        dx_back_b = to_tokens(dx_b)
        wgrad_two = jnp.einsum('ecf,ecd->efd', mid_act, grad_recv, preferred_element_type=jnp.float32).astype(jnp.bfloat16)

        def wgrad(lo, part):
            return jnp.einsum('ecd,ecf->edf', recv_rows[lo : lo + part.shape[0]], part, preferred_element_type=jnp.float32).astype(jnp.bfloat16)

        wgrad_one = jnp.concatenate([wgrad(0, u_a), wgrad(cut, u_b)])
        wgrad_three = jnp.concatenate([wgrad(0, v_a), wgrad(cut, v_b)])

        cols = jnp.concatenate([to_cols(position), to_cols(w_hi), to_cols(w_mid), to_cols(w_low)], axis=2)
        half = group_size // 2
        routed_a, dots_a = combine(cols, back_out, 0, half, dot_back)
        routed_b, dots_b = combine(cols, back_out, half, half, dot_back)
        routed, dots = routed_a + routed_b, dots_a + dots_b
        hidden_out = (hidden.astype(jnp.float32) + shared_out + routed).astype(jnp.bfloat16)
        route_dot = dots[:, :num_experts]
        mean_term = jnp.sum(route_dot * weights, axis=1, keepdims=True) / ROUTE_SCALE
        grad_pick = ROUTE_SCALE / pick_sum * (route_dot - mean_term) * scores * (1.0 - scores)
        grad_logits = jnp.where(chosen, grad_pick, 0.0).astype(jnp.bfloat16)
        router_part = jnp.einsum('td,te->de', hidden, grad_logits, preferred_element_type=jnp.float32)
        gate_dx = jnp.einsum('te,de->td', grad_logits, w_router, preferred_element_type=jnp.float32)

        dx_routed_a = combine(part_cols(position, 0, cut), dx_back_a, 0, cut * group_size // segs)[0]
        dx_routed_b = combine(part_cols(position, cut, local_experts), dx_back_b, 0, (local_experts - cut) * group_size // segs)[0]
        grad_hidden = (grad_out.astype(jnp.float32) + shared_dx + gate_dx + dx_routed_a + dx_routed_b).astype(jnp.bfloat16)
        grad_router = jnp.sum(lax.all_gather(router_part, 'ep', axis=0), axis=0)
        return (hidden_out, grad_hidden, grad_router, wgrad_one, wgrad_three, wgrad_two, grad_shared_one, grad_shared_three, grad_shared_two)

    return jax.shard_map(layer, mesh=mesh, in_specs=(row_spec, row_spec, row_spec, copy_spec, expert_spec, expert_spec, expert_spec, copy_spec, copy_spec, copy_spec), out_specs=(row_spec, row_spec, copy_spec, expert_spec, expert_spec, expert_spec, copy_spec, copy_spec, copy_spec), check_vma=False)
```

time: 3580 us -> 2340 us (0.65)
  local copies, waits for them, and re-layouts: 1220 us -> 67.5 us
  Pallas kernels: 0 us -> 996 us
  blocking collectives: 437 us -> 0 us
  matrix products: 715 us -> 354 us
  waiting for transfers between devices: 999 us -> 840 us
  other arithmetic: 162 us -> 31.8 us
    gather x14 -> x0, local copies, waits for them, and re-layouts: 1030 us -> none  [the longest x2 332 us: local_step(): jnp.take(dx_back, slot_ids, axis=0, mode='fill', fill_value=0)]
    pallas_call x0 -> x9, Pallas kernels: none -> 996 us  [the longest x4 443 us: combine(): pl.pallas_call(functools.partial(combine_kernel, weighted, first), grid=(...]
    all_to_all x3 -> x5, waiting for transfers between devices: 999 us -> 320 us  [the longest x3 320 us: to_tokens(): return lax.all_to_all(rows, 'ep', 0, 0).reshape(-1, capacity, d_model)]
    all_to_all x1 -> x0, blocking collectives: 437 us -> none  [local_step(): recv_rows = lax.all_to_all(send_rows, 'ep', 0, 0)]
    dot_general x13 -> x9, matrix products: 568 us -> 197 us  [the longest x4 118 us: wgrad(): jnp.einsum('ecd,ecf->edf', recv_rows[lo:lo + part.shape[0]], part, prefer...]
    all_gather x0 -> x3, waiting for transfers between devices: none -> 323 us  [the longest x1 277 us: layer(): all_hidden = lax.all_gather(hidden, 'ep', axis=0, tiled=True)]
    psum x1, waiting for transfers between devices: 0.01 us -> 195 us  [layer(): lax.psum((sgrad_one, sgrad_three, sgrad_two), 'ep')]
    scatter x2 -> x0, local copies, waits for them, and re-layouts: 91 us -> none  [the longest x1 45.6 us: slot_tables(): jnp.zeros((num_experts * capacity,), jnp.float32).at[flat_slots]]
  transfers between devices with their start and end apart: 4 -> 9, of which waited for: 3 -> 4; matrix products, arithmetic and copies ran while one was open for 20% -> 14% of each run, Pallas kernels for 0% -> 39%
where the time goes in v1:
time: 2340 us; the launch traced here: 2330 us
  Pallas kernels  996 us (43%)
  waiting for transfers between devices  840 us (36%)
  matrix products  354 us (15%)
  local copies, waits for them, and re-layouts  67.5 us (3%)
  other arithmetic  31.8 us (1%)
    pallas_call x4, Pallas kernels, combine(): pl.pallas_call(functools.partial(combine_kernel, weighted, first), grid=(...  443 us
    all_to_all x3, waiting for transfers between devices, to_tokens(): return lax.all_to_all(rows, 'ep', 0, 0).reshape(-1, capacity, d_model)  320 us
    all_gather x1, waiting for transfers between devices, layer(): all_hidden = lax.all_gather(hidden, 'ep', axis=0, tiled=True)  277 us
    pallas_call x2, Pallas kernels, expert_backward(): pl.pallas_call(backward_kernel, grid=(count, group_size // groups), in_sp...  202 us
    psum x1, waiting for transfers between devices, layer(): lax.psum((sgrad_one, sgrad_three, sgrad_two), 'ep')  195 us
    pallas_call x1, Pallas kernels, expert_forward(): pl.pallas_call(forward_kernel, grid=(local_experts, group_size // groups)...  164 us
    dot_general x4, matrix products, wgrad(): jnp.einsum('ecd,ecf->edf', recv_rows[lo:lo + part.shape[0]], part, prefer...  118 us
    pallas_call x1, Pallas kernels, select_grads(): pl.pallas_call(select_grad_kernel, grid=(group_size,), in_specs=[pl.Block...  98 us
  transfers between devices with their start and end apart: 9, of which 4 were waited for; matrix products, arithmetic and copies ran while one was open for 14% of the time, Pallas kernels for 39%

profile of v1, /device:TPU:11, one launch (start us, length us, event | category | flops | bytes accessed | tf_op | source)
XLA Modules:
  0.0 2325.9 jit_solution(8939212508319349520)
XLA Ops:
  7.2 15.9 fusion.37
  23.1 15.9 fusion.38
  39.1 27.9 %multiply_convert_fusion = (bf16[2048,1792]{1,0:T(8,128)(2,1)}, bf16[2048,1792]{1,0:T(8,128)(2,1)}, bf16[2048,1792]{1,0:T(8,128)(2,1)}) fusion(f32[2048,1792]{1,0:T(8,128)} %fusion.37, f32[2048,1792]{1,0:T(8,128)} %fusion.38, bf16[2048,1280]{1,0:T(8,128)(2,1)} %param.11, bf16[1792,1280]{1,0:T(8,128)(2,1)} %param.19), kind=kOutput, calls=%fused_computation.2 | convolution fusion | flops 9450291200 | bytes 61210624 | tf_op jit(solution)/shard_map/td,fd->tf/dot_general | solution.py:310
  67.0 16.1 convolution_bitcast_fusion
  83.1 15.0 convolution_bitcast_fusion.1
  98.1 13.1 fusion.41
  111.3 0.7 all-gather.7.cloned.1.call-update
  112.1 0.7 all-gather.5.cloned.1.call-update
  112.9 6.9 select_reduce_fusion
  119.8 5.8 fusion.34
  125.7 2.3 bitcast_select_fusion.1
  128.0 0.3 copy.80
  128.4 0.3 copy.82
  128.9 1.2 pad_maximum_fusion.3
  130.2 4.5 all-to-all-start
  134.6 16.9 fusion.39
  151.5 15.9 fusion.40
  167.5 0.3 copy.73
  167.9 1.6 copy.76
  169.7 1.5 copy.77
  171.3 0.9 reshape.91
  172.6 0.9 reshape.92
  173.5 1.8 pad_maximum_fusion.2
  175.3 8.5 copy.84.refs_0_
  184.1 6.7 copy.86
  190.8 0.4 slice_reduce_fusion.1
  191.2 2.7 copy.87
  193.9 195.4 %all-reduce.4.cloned.1.call-done = (f32[1280,1792]{0,1:T(8,128)}, f32[1280,1792]{0,1:T(8,128)}, f32[1792,1280]{1,0:T(8,128)}) async-done(((f32[1280,1792]{0,1:T(8,128)}, f32[1280,1792]{0,1:T(8,128)}, f32[1792,1280]{1,0:T(8,128)}), (f32[1280,1792]{0,1:T(8,128)}, f32[1280,1792]{0,1:T(8,128)}, f32[1792,1280]{1,0:T(8,128)})) %all-reduce.4.cloned.1.call-update) | async-done | bytes 27525136 | tf_op jit(solution)/shard_map/psum | solution.py:357
  389.4 10.8 copy.91
  400.2 11.5 copy.92
  411.7 276.7 %all-gather.7.cloned.1.call-done.rows_ref = bf16[32768,1280]{1,0:T(8,128)(2,1)} async-done(((bf16[2048,1280]{1,0:T(8,128)(2,1)}), bf16[32768,1280]{1,0:T(8,128)(2,1)}) %all-gather.7.cloned.1.call-update) | async-done | bytes 83886096 | tf_op jit(solution)/shard_map/all_gather | solution.py:332
  688.4 88.4 %shard_map.169.x_ref = bf16[4,3840,1280]{2,1,0:T(8,128)(2,1)} custom-call(f32[16,8,2048]{2,1,0:T(8,128)} %all-to-all-done.pos_ref, bf16[32768,1280]{1,0:T(8,128)(2,1)} %all-gather.7.cloned.1.call-done.rows_ref), custom_call_target="tpu_custom_call" | custom-call | flops 80530636800 | bytes 123207680 | tf_op jit(solution)/shard_map/pallas_call | solution.py:63
  776.8 164.1 %shard_map.170 = (f32[4,3840,896]{2,1,0:T(8,128)}, f32[4,3840,896]{2,1,0:T(8,128)}, bf16[4,3840,896]{2,1,0:T(8,128)(2,1)}, bf16[16,4,240,1280]{3,2,1,0:T(8,128)(2,1)}) custom-call(bf16[4,3840,1280]{2,1,0:T(8,128)(2,1)} %shard_map.169.x_ref, bf16[4,1280,896]{2,1,0:T(8,128)(2,1)} %one_ref.5, bf16[4,1280,896]{2,1,0:T(8,128)(2,1)} %three_ref.5, ...), custom_call_target="tpu_custom_call" | custom-call | flops 105696460800 | bytes 216268800 | tf_op jit(solution)/shard_map/pallas_call | solution.py:152
  941.0 46.3 %all-gather.5.cloned.1.call-done.rows_ref = bf16[32768,1280]{1,0:T(8,128)(2,1)} async-done(((bf16[2048,1280]{1,0:T(8,128)(2,1)}), bf16[32768,1280]{1,0:T(8,128)(2,1)}) %all-gather.5.cloned.1.call-update) | async-done | bytes 83886096 | tf_op jit(solution)/shard_map/all_gather | solution.py:333
  987.3 98.0 %shard_map.171 = (bf16[4,3840,1280]{2,1,0:T(8,128)(2,1)}, f32[16,960,128]{2,1,0:T(8,128)}) custom-call(f32[16,8,2048]{2,1,0:T(8,128)} %all-to-all-done.pos_ref, bf16[32768,1280]{1,0:T(8,128)(2,1)} %all-gather.5.cloned.1.call-done.rows_ref, bf16[16,4,240,1280]{3,2,1,0:T(8,128)(2,1)} %get-tuple-element.25.outs_ref), custom_call_target="tpu_custom_call" | custom-call | flops 80530636800 | bytes 201850880 | tf_op jit(solution)/shard_map/pallas_call | solution.py:106
  1085.3 5.5 slice_reduce_fusion
  1090.7 0.7 all_to_all.24
  1091.4 4.3 all-to-all-start.1
  1095.7 54.7 %shard_map.176 = (bf16[1,3840,896]{2,1,0:T(8,128)(2,1)}, bf16[1,3840,896]{2,1,0:T(8,128)(2,1)}, bf16[16,1,240,1280]{3,2,1,0:T(8,128)(2,1)}) custom-call(bf16[4,3840,1280]{2,1,0:T(8,128)(2,1)} %get-tuple-element.31.q_ref, f32[4,3840,896]{2,1,0:T(8,128)} %get-tuple-element.32.pre_one_ref, f32[4,3840,896]{2,1,0:T(8,128)} %get-tuple-element.33.pre_three_ref, ...), custom_call_target="tpu_custom_call" | custom-call | flops 26424115200 | bytes 60948480 | tf_op jit(solution)/shard_map/pallas_call | solution.py:203
  1150.4 16.0 fusion.12
  1166.4 0.6 copy-done.7
  1167.0 4.2 all-to-all-start.4
  1171.2 16.0 fusion.15
  1187.2 147.3 %shard_map.174 = (bf16[3,3840,896]{2,1,0:T(8,128)(2,1)}, bf16[3,3840,896]{2,1,0:T(8,128)(2,1)}, bf16[16,3,240,1280]{3,2,1,0:T(8,128)(2,1)}) custom-call(bf16[4,3840,1280]{2,1,0:T(8,128)(2,1)} %get-tuple-element.31.q_ref, f32[4,3840,896]{2,1,0:T(8,128)} %get-tuple-element.32.pre_one_ref, f32[4,3840,896]{2,1,0:T(8,128)} %get-tuple-element.33.pre_three_ref, ...), custom_call_target="tpu_custom_call" | custom-call | flops 79272345600 | bytes 182845440 | tf_op jit(solution)/shard_map/pallas_call | solution.py:203
  1334.5 5.0 all-to-all-start.2
  1339.6 42.5 %convolution_convert_fusion.1 = bf16[3,1280,896]{2,1,0:T(8,128)(2,1)} fusion(bf16[4,3840,1280]{2,1,0:T(8,128)(2,1)} %shard_map.169.x_ref, bf16[3,3840,896]{2,1,0:T(8,128)(2,1)} %get-tuple-element.38), kind=kOutput, calls=%fused_computation.20 | convolution fusion | flops 26427555840 | bytes 66846720 | tf_op jit(solution)/shard_map/ecd,ecf->edf/dot_general | solution.py:373
  1382.1 43.0 %convolution_convert_fusion.2 = bf16[3,1280,896]{2,1,0:T(8,128)(2,1)} fusion(bf16[4,3840,1280]{2,1,0:T(8,128)(2,1)} %shard_map.169.x_ref, bf16[3,3840,896]{2,1,0:T(8,128)(2,1)} %get-tuple-element.36), kind=kOutput, calls=%fused_computation.21 | convolution fusion | flops 26427555840 | bytes 66846720 | tf_op jit(solution)/shard_map/ecd,ecf->edf/dot_general | solution.py:373
  1425.1 13.7 pad_maximum_fusion
  1438.8 44.1 %convolution_convert_fusion = bf16[4,896,1280]{2,1,0:T(8,128)(2,1)} fusion(bf16[4,3840,896]{2,1,0:T(8,128)(2,1)} %get-tuple-element.40, bf16[4,3840,1280]{2,1,0:T(8,128)(2,1)} %get-tuple-element.31.q_ref), kind=kOutput, calls=%fused_computation.7 | convolution fusion | flops 35236741120 | bytes 76021760 | tf_op jit(solution)/shard_map/ecf,ecd->efd/dot_general | solution.py:370
  1483.2 0.6 pad.4.refs_1_
  1483.8 319.7 %all-to-all-done.2 = bf16[16,960,1280]{2,1,0:T(8,128)(2,1)} async-done(((bf16[16,960,1280]{2,1,0:T(8,128)(2,1)}), bf16[16,960,1280]{2,1,0:T(8,128)(2,1)}, u32[]{:S(2)}, u32[]{:S(2)}) %all-to-all-start.2) | async-done | bytes 39321632 | tf_op jit(solution)/shard_map/all_to_all | solution.py:353
  1803.5 4.4 all-to-all-start.3
  1807.9 34.7 %shard_map.177 = f32[2048,1280]{1,0:T(8,128)} custom-call(f32[4,2048,4]{2,1,0:T(8,128)} %bitcast.123, bf16[16,240,1280]{2,1,0:T(8,128)(2,1)} %all-to-all-done.4.refs_1_), custom_call_target="tpu_custom_call" | custom-call | flops 21474836480 | bytes 20316160 | tf_op jit(solution)/shard_map/pallas_call | solution.py:288
  1842.6 159.1 %shard_map.173 = (f32[2048,1280]{1,0:T(8,128)}, f32[2048,128]{1,0:T(8,128)}) custom-call(f32[16,2048,16]{2,1,0:T(8,128)} %copy.84.refs_0_, f32[16,4,256]{2,1,0:T(4,128)} %pad.4.refs_1_, bf16[64,240,1280]{2,1,0:T(8,128)(2,1)} %bitcast.13.refs_2_), custom_call_target="tpu_custom_call" | custom-call | flops 128849018880 | bytes 30146560 | tf_op jit(solution)/shard_map/pallas_call | solution.py:288
  2001.8 159.5 %shard_map.172 = (f32[2048,1280]{1,0:T(8,128)}, f32[2048,128]{1,0:T(8,128)}) custom-call(f32[16,2048,16]{2,1,0:T(8,128)} %copy.84.refs_0_, f32[16,4,256]{2,1,0:T(4,128)} %pad.4.refs_1_, bf16[64,240,1280]{2,1,0:T(8,128)(2,1)} %bitcast.13.refs_2_), custom_call_target="tpu_custom_call" | custom-call | flops 128849018880 | bytes 30146560 | tf_op jit(solution)/shard_map/pallas_call | solution.py:288
  2161.4 5.6 multiply_reduce_fusion
  2167.0 5.5 select_convert_fusion
  2172.5 4.1 convolution_bitcast_fusion.2
  2176.6 89.9 %shard_map.175 = f32[2048,1280]{1,0:T(8,128)} custom-call(f32[12,2048,4]{2,1,0:T(8,128)} %bitcast.118, bf16[48,240,1280]{2,1,0:T(8,128)(2,1)} %bitcast.16.refs_1_), custom_call_target="tpu_custom_call" | custom-call | flops 64424509440 | bytes 39976960 | tf_op jit(solution)/shard_map/pallas_call | solution.py:288
  2266.4 18.2 add_convert_fusion
  2284.7 20.6 add_convert_fusion.1
  2305.3 4.1 copy.99
  2309.4 1.6 bitcast_reduce_fusion
  2311.0 7.8 copy.103
  (81 shorter events, 1.9 us)
Async XLA Ops:
  7.2 105.7 %copy-start = (bf16[1280,64]{0,1:T(8,128)(2,1)S(1)}, bf16[1280,64]{0,1:T(8,128)(2,1)}, u32[]{:S(2)}) copy-start(bf16[1280,64]{0,1:T(8,128)(2,1)} %param.13) | copy-start | bytes 491524
  7.2 382.2 %all-reduce.4.cloned.1.call-start = ((), (), s32[]{:S(2)}) async-start(), calls=%async_computation.8 | async-start | bytes 55050240 | tf_op jit(solution)/shard_map/psum | solution.py:357
  67.0 16.1 copy-start.24
  67.0 31.1 %slice-start = ((s8[5242880]{0:T(1024)(128)(4,1)}), s8[4194304]{0:T(1024)(128)(4,1)S(1)}, s32[]{:S(2)}) async-start(s8[5242880]{0:T(1024)(128)(4,1)} %bitcast.116), calls=%async_computation.9 | async-start | bytes 8388608
  67.0 31.1 %slice-start.2 = ((s8[7340032]{0:T(1024)(128)(4,1)}), s8[4194304]{0:T(1024)(128)(4,1)S(1)}, s32[]{:S(2)}) async-start(s8[7340032]{0:T(1024)(128)(4,1)} %bitcast.157), calls=%async_computation.11 | async-start | bytes 8388608
  83.1 15.0 slice-start.1
  83.1 15.0 slice-start.3
  111.3 1.5 copy-start.23
  111.3 577.1 %all-gather.7.cloned.1.call-start = ((), (), s32[]{:S(2)}) async-start(), calls=%async_computation.6 | async-start | bytes 89128960 | tf_op jit(solution)/shard_map/all_gather | solution.py:332
  112.0 875.2 %all-gather.5.cloned.1.call-start = ((), (), s32[]{:S(2)}) async-start(), calls=%async_computation.5 | async-start | bytes 89128960 | tf_op jit(solution)/shard_map/all_gather | solution.py:333
  112.8 12.8 copy-start.9
  112.8 12.8 copy-start.11
  112.9 12.8 copy-start.13
  112.9 12.8 copy-start.15
  112.9 12.8 copy-start.17
  112.9 12.8 copy-start.19
  119.8 5.9 copy-start.1
  119.8 5.9 copy-start.21
  130.2 281.6 %all-to-all-start = ((f32[16,8,2048]{2,1,0:T(8,128)}), f32[16,8,2048]{2,1,0:T(8,128)}, u32[]{:S(2)}, u32[]{:S(2)}) async-start(f32[16,8,2048]{2,1,0:T(8,128)} %pad_maximum_fusion.3), calls=%async_computation | async-start | bytes 2097152 | tf_op jit(solution)/shard_map/all_to_all | solution.py:338
  151.5 15.9 copy-start.6
  151.5 20.7 copy-start.5
  1091.4 75.0 %all-to-all-start.1 = ((f32[16,1,960]{2,1,0:T(1,128)}), f32[16,1,960]{2,1,0:T(1,128)S(1)}, u32[]{:S(2)}, u32[]{:S(2)}) async-start(f32[16,1,960]{2,1,0:T(1,128)} %all_to_all.24), calls=%async_computation.1 | async-start | bytes 131072 | tf_op jit(solution)/shard_map/all_to_all | solution.py:362
  1166.4 0.6 copy-start.7
  1167.0 167.5 %all-to-all-start.4 = ((bf16[16,240,1280]{2,1,0:T(8,128)(2,1)}), bf16[16,240,1280]{2,1,0:T(8,128)(2,1)}, u32[]{:S(2)}, u32[]{:S(2)}) async-start(bf16[16,240,1280]{2,1,0:T(8,128)(2,1)} %bitcast.119), calls=%async_computation.4 | async-start | bytes 19660800 | tf_op jit(solution)/shard_map/all_to_all | solution.py:353
  1334.5 468.9 %all-to-all-start.2 = ((bf16[16,960,1280]{2,1,0:T(8,128)(2,1)}), bf16[16,960,1280]{2,1,0:T(8,128)(2,1)}, u32[]{:S(2)}, u32[]{:S(2)}) async-start(bf16[16,960,1280]{2,1,0:T(8,128)(2,1)} %bitcast.114), calls=%async_computation.2 | async-start | bytes 78643200 | tf_op jit(solution)/shard_map/all_to_all | solution.py:353
  1382.1 43.0 %copy-start.4 = (bf16[1,1280,896]{2,1,0:T(8,128)(2,1)S(1)}, bf16[1,1280,896]{2,1,0:T(8,128)(2,1)}, u32[]{:S(2)}) copy-start(bf16[1,1280,896]{2,1,0:T(8,128)(2,1)} %fusion.12) | copy-start | bytes 6881284
  1438.8 44.1 %copy-start.8 = (f32[16,1,960]{2,1,0:T(1,128)S(1)}, f32[16,1,960]{2,1,0:T(1,128)}, u32[]{:S(2)}) copy-start(f32[16,1,960]{2,1,0:T(1,128)} %copy-done.7) | copy-start | bytes 184324
  1803.5 373.1 %all-to-all-start.3 = ((bf16[16,720,1280]{2,1,0:T(8,128)(2,1)}), bf16[16,720,1280]{2,1,0:T(8,128)(2,1)}, u32[]{:S(2)}, u32[]{:S(2)}) async-start(bf16[16,720,1280]{2,1,0:T(8,128)(2,1)} %bitcast.115), calls=%async_computation.3 | async-start | bytes 58982400 | tf_op jit(solution)/shard_map/all_to_all | solution.py:353
  1807.9 497.4 %all-gather.9.cloned.1.call-start = ((), (), s32[]{:S(2)}) async-start(), calls=%async_computation.7 | async-start | bytes 5570560 | tf_op jit(solution)/shard_map/all_gather | solution.py:394
  2001.7 159.6 %copy-start.2 = (f32[2048,64]{1,0:T(8,128)S(1)}, f32[2048,64]{1,0:T(8,128)}, u32[]{:S(2)}) copy-start(f32[2048,64]{1,0:T(8,128)} %copy-done.1) | copy-start | bytes 1572868
  2001.7 159.6 %copy-start.3 = (f32[2048,128]{1,0:T(8,128)S(1)}, f32[2048,128]{1,0:T(8,128)}, u32[]{:S(2)}) copy-start(f32[2048,128]{1,0:T(8,128)} %get-tuple-element.30) | copy-start | bytes 3145732
  2001.7 159.6 %copy-start.10 = (s32[2048,1]{0,1:T(1,128)S(1)}, s32[2048,1]{0,1:T(1,128)}, u32[]{:S(2)}) copy-start(s32[2048,1]{0,1:T(1,128)} %copy-done.9) | copy-start | bytes 24580
  2001.7 159.6 %copy-start.12 = (s32[2048,1]{0,1:T(1,128)S(1)}, s32[2048,1]{0,1:T(1,128)}, u32[]{:S(2)}) copy-start(s32[2048,1]{0,1:T(1,128)} %copy-done.11) | copy-start | bytes 24580
  2001.7 159.6 %copy-start.14 = (s32[2048,1]{0,1:T(1,128)S(1)}, s32[2048,1]{0,1:T(1,128)}, u32[]{:S(2)}) copy-start(s32[2048,1]{0,1:T(1,128)} %copy-done.13) | copy-start | bytes 24580
  2001.8 159.6 %copy-start.16 = (s32[2048,1]{0,1:T(1,128)S(1)}, s32[2048,1]{0,1:T(1,128)}, u32[]{:S(2)}) copy-start(s32[2048,1]{0,1:T(1,128)} %copy-done.15) | copy-start | bytes 24580
  2001.8 159.6 %copy-start.18 = (s32[2048,1]{0,1:T(1,128)S(1)}, s32[2048,1]{0,1:T(1,128)}, u32[]{:S(2)}) copy-start(s32[2048,1]{0,1:T(1,128)} %copy-done.17) | copy-start | bytes 24580
  2001.8 159.6 %copy-start.20 = (s32[2048,1]{0,1:T(1,128)S(1)}, s32[2048,1]{0,1:T(1,128)}, u32[]{:S(2)}) copy-start(s32[2048,1]{0,1:T(1,128)} %copy-done.19) | copy-start | bytes 24580
  2001.8 159.6 %copy-start.22 = (f32[2048]{0:T(1024)S(1)}, f32[2048]{0:T(1024)}, u32[]{:S(2)}) copy-start(f32[2048]{0:T(1024)} %copy-done.21) | copy-start | bytes 24580
Sparse Core Ops, SparseCore 0:
  111.4 277.9 all-reduce.3
  391.6 296.7 all-gather.6
  690.7 296.4 all-gather.4
  2176.7 40.0 all-gather.8
